TPU v7x, 32 devices: a whole 2x2x4 slice. The times are simulated.
32 devices in a mesh: groups: 2 (over y), ra: 4 (over z), dec: 2 (over x), rep: 2 (over core).
Axes of the slice: x: 2, y: 2, z: 4, core: 2. Of those that a mesh axis runs over, the one named last changes fastest.
Arguments:
- tiles: bfloat16 [2048, 16384], P(('groups', 'ra', 'dec', 'rep')), parts along dimension 0, may hold values from -6 to 6
- tile_route: int32 [2048, 1], P(('groups', 'ra', 'dec', 'rep')), parts along dimension 0, may hold values from 0 to 3; in each aligned block of 64 rows (0 to 63, 64 to 127, ...) at most 32 rows name the same one
- tile_visit: int32 [2048], P(('groups', 'ra', 'dec', 'rep')), parts along dimension 0, may hold values from 0 to 7
- tile_offset: int32 [2048], P(('groups', 'ra', 'dec', 'rep')), parts along dimension 0, may hold values from 0 to 64
- tile_weight: float32 [2048], P(('groups', 'ra', 'dec', 'rep')), parts along dimension 0, may hold values from 0.1 to 10
- resampling: bfloat16 [16, 2, 128, 128], P('groups'), parts along dimension 0, may hold values from 0 to 0.17675781
- psf_taps: float32 [16, 2, 5], P('groups'), parts along dimension 0, may hold values from 0.1 to 1
Outputs:
- coadd: float32 [512, 512], P(('groups', 'dec'), 'ra'), parts along dimension 0
- weight_map: float32 [512, 512], P(('groups', 'dec'), 'ra'), parts along dimension 0
There are 2 independent parts, one for each index of `groups`. A program takes and returns all parts, laid end to end along the dimension named above; each array names one. Nothing has to cross between parts.
Inputs may be any that keep to these rules, and one draw needn't show every extreme that they name: `tile_route`: among the tiles of one device, at most 32 name the same RA band; in every draw some RA band is named by exactly 32 tiles of some device.
All inputs are finite; a program needn't handle non-finite values.
Results may differ from a plain program's by a relative error of at most 0.0019.
Values may be sent and summed in bfloat16 or wider, within the bound.
A program may use at most 64 MiB of HBM per device.

v0:
```python
import math

import jax
import jax.numpy as jnp
from jax import lax
from jax.sharding import PartitionSpec as P

PIX = 128
MARGIN = 32


def padded_2(x, sides, width):
    for axis, dim in sides:
        count, length = (lax.axis_size(axis), x.shape[dim])
        up = [(i, (i + 1) % count) for i in range(count - 1)]
        down = [(j, i) for i, j in up]
        last = lax.slice_in_dim(x, length - width, length, axis=dim)
        leading = lax.slice_in_dim(x, 0, width, axis=dim)
        before = lax.ppermute(last, axis, up)
        after = lax.ppermute(leading, axis, down)
        x = jnp.concatenate([before, x, after], axis=dim)
    return x


def convolve(image, row_taps, col_taps):
    height = image.shape[1]
    width = image.shape[2]
    padded = jnp.pad(image, ((0, 0), (2, 2), (0, 0)))
    along = jnp.zeros_like(image)
    for k in range(5):
        along = along + row_taps[:, k][:, None, None] * padded[:, k : k + height, :]
    padded = jnp.pad(along, ((0, 0), (0, 0), (2, 2)))
    result = jnp.zeros_like(image)
    for k in range(5):
        result = result + col_taps[:, k][:, None, None] * padded[:, :, k : k + width]
    return result


def render(tiles, visit, offset, resampling, psf_taps):
    count = tiles.shape[0]
    canvas_rows = PIX + 2 * MARGIN
    grid = tiles.reshape(count, PIX, PIX)
    col_maps = resampling[visit, 1]
    mid = jnp.einsum("nab,nkb->nak", grid, col_maps, preferred_element_type=jnp.float32).astype(
        jnp.bfloat16
    )
    row_pad = jnp.pad(resampling[:, 0], ((0, 0), (2 * MARGIN, 2 * MARGIN), (0, 0)))

    def place(v, o):
        start = 2 * MARGIN - o
        return lax.dynamic_slice(row_pad, (v, start, jnp.int32(0)), (1, canvas_rows, PIX))[0]

    rows = jax.vmap(place)(visit, offset)
    image = jnp.einsum("nia,nak->nik", rows, mid, preferred_element_type=jnp.float32)
    matched = convolve(image, psf_taps[visit, 0], psf_taps[visit, 1])
    row_sums = jnp.sum(rows.astype(jnp.float32), axis=2)
    col_sums = jnp.sum(col_maps.astype(jnp.float32), axis=2)
    return (matched, row_sums, col_sums)


def accumulate(tiles, visit, offset, shares, resampling, psf_taps):
    count = tiles.shape[0]
    block = math.gcd(count, 128)
    canvas_rows = PIX + 2 * MARGIN
    members = shares.shape[1]

    def step(carry, index):
        num_sum, den_sum = carry
        matched, row_sums, col_sums = render(tiles, visit, offset, resampling, psf_taps)
        num_sum = num_sum + jnp.einsum(
            "tg,tik->gik", shares, matched, precision=lax.Precision.HIGHEST
        )
        den_sum = den_sum + jnp.einsum(
            "tg,ti,tk->gik", shares, row_sums, col_sums, precision=lax.Precision.HIGHEST
        )
        return ((num_sum, den_sum), None)

    zeros = jnp.zeros((members, canvas_rows, PIX), jnp.float32)
    (num_sum, den_sum), _ = lax.scan(
        step, (zeros, zeros), jnp.arange(count // block, dtype=jnp.int32)
    )
    return (num_sum, den_sum)


def on_device(tiles, tile_route, tile_visit, tile_offset, tile_weight, resampling, psf_taps):
    bands = lax.axis_size("ra")
    canvas_rows = PIX + 2 * MARGIN
    target = tile_route[:, 0]
    member = (target[:, None] == jnp.arange(bands, dtype=jnp.int32)[None, :]).astype(jnp.int32)
    shares = member.astype(jnp.float32) * tile_weight[:, None]
    num_sum, den_sum = accumulate(tiles, tile_visit, tile_offset, shares, resampling, psf_taps)
    num_sum, den_sum = (
        lax.psum_scatter(num_sum, "ra", scatter_dimension=0, tiled=True),
        lax.psum_scatter(den_sum, "ra", scatter_dimension=0, tiled=True),
    )
    num_sum, den_sum = lax.psum((num_sum[0], den_sum[0]), "rep")
    stacked = jnp.stack([num_sum, den_sum])
    padded = padded_2(stacked, (("dec", 1),), MARGIN)
    core = stacked[:, MARGIN : MARGIN + PIX]
    core = core.at[:, :MARGIN].add(padded[:, :MARGIN])
    core = core.at[:, PIX - MARGIN :].add(padded[:, MARGIN + canvas_rows :])
    coadd = core[0] / (core[1] + 1.0)
    return (coadd, core[1])


def solution(mesh):
    in_specs = (
        P(("groups", "ra", "dec", "rep"), None),
        P(("groups", "ra", "dec", "rep"), None),
        P(("groups", "ra", "dec", "rep")),
        P(("groups", "ra", "dec", "rep")),
        P(("groups", "ra", "dec", "rep")),
        P("groups", None, None, None),
        P("groups", None, None),
    )
    out_specs = (P(("groups", "dec"), "ra"), P(("groups", "dec"), "ra"))
    return jax.shard_map(
        on_device, mesh=mesh, in_specs=in_specs, out_specs=out_specs, check_vma=False
    )
```

profile of v0, /device:TPU:0, one launch (start us, length us, event | category | flops | bytes accessed | tf_op | source)
XLA Modules:
  0.0 156.3 jit_solution(10803857297674921332)
XLA Ops:
  7.9 0.8 copy.23
  8.6 1.0 slice.147
  9.6 2.0 %gather_fusion.3 = bf16[64,128,128]{2,1,0:T(8,128)(2,1)S(1)} fusion(bf16[8,2,128,128]{3,2,1,0:T(8,128)(2,1)} %param.16, s32[64]{0:T(128)S(1)} %get-tuple-element.67), kind=kCustom, calls=%fused_computation.3 | custom fusion | bytes 4194816 | tf_op jit(solution)/shard_map/while/body/eval_jaxpr/gather | solution.py:43
  11.6 0.8 gather_fusion
  12.4 0.8 gather_fusion.1
  13.2 0.7 shift-left_or_fusion
  14.5 3.6 %copy.33 = bf16[8,8,128,128]{3,2,1,0:T(8,128)(2,1)} copy(bf16[8,8,128,128]{3,1,2,0:T(8,128)(2,1)} %bitcast.24) | data formatting | bytes 4194304
  18.2 14.4 %gather_fusion.2 = bf16[64,192,128]{2,0,1:T(8,128)(2,1)} fusion(bf16[8,256,128]{2,0,1:T(8,128)(2,1)S(1)} %pad.21, s32[64]{0:T(128)S(1)} %shift-left_or_fusion), kind=kCustom, calls=%fused_computation.2 | custom fusion | bytes 6292224 | tf_op jit(solution)/shard_map/while/body/eval_jaxpr/vmap()/gather | solution.py:51
  32.6 10.0 %fusion.11 = f32[64,192,128]{2,1,0:T(8,128)} fusion(bf16[64,192,128]{2,0,1:T(8,128)(2,1)} %gather_fusion.2, bf16[64,128,128]{2,1,0:T(8,128)(2,1)S(1)} %gather_fusion.3, bf16[64,128,128]{2,1,0:T(8,128)(2,1)} %bitcast.23), kind=kOutput, calls=%fused_computation.23 | convolution fusion | flops 672137216 | bytes 13631488 | tf_op jit(solution)/shard_map/while/body/eval_jaxpr/nia,nak->nik/dot_general | solution.py:54
  42.6 15.5 %multiply_add_fusion = f32[64,192,128]{2,1,0:T(8,128)S(1)} fusion(f32[64,192,128]{2,1,0:T(8,128)} %fusion.11, f32[64]{0:T(128)S(1)} %get-tuple-element.62, f32[64]{0:T(128)S(1)} %get-tuple-element.59, f32[64]{0:T(128)S(1)} %get-tuple-element.60, f32[64]{0:T(128)S(1)} %get-tuple-element.61, f32[64]{0:T(128)S(1)} %get-tuple-element.58), kind=kLoop, calls=%fused_computation.19 | loop fusion | flops 14155776 | bytes 12584192 | tf_op jit(solution)/shard_map/while/body/eval_jaxpr/add | solution.py:31
  58.2 8.5 %fusion.4 = f32[64,192,128]{2,1,0:T(8,128)S(1)} fusion(f32[64,192,128]{2,1,0:T(8,128)S(1)} %multiply_add_fusion, f32[64]{0:T(128)S(1)} %get-tuple-element.57, f32[64]{0:T(128)S(1)} %get-tuple-element.54, f32[64]{0:T(128)S(1)} %get-tuple-element.55, f32[64]{0:T(128)S(1)} %get-tuple-element.56, f32[64]{0:T(128)S(1)} %get-tuple-element.53), kind=kLoop, calls=%fused_computation.12 | loop fusion | flops 14155776 | bytes 12584192 | tf_op jit(solution)/shard_map/while/body/eval_jaxpr/add | solution.py:35
  66.7 6.5 %fusion.8 = f32[4,192,128]{2,0,1:T(4,128)S(1)} fusion(f32[64,192,128]{2,1,0:T(8,128)S(1)} %fusion.4, f32[64]{0:T(128)S(1)} %copy-done.2, s32[64]{0:T(128)S(1)} %bitcast.26), kind=kOutput, calls=%fused_computation.16 | convolution fusion | flops 75498496 | bytes 6685184 | tf_op jit(solution)/shard_map/while/body/eval_jaxpr/tg,tik->gik/dot_general | solution.py:70
  73.1 0.8 copy.28
  74.2 2.2 %convert_reduce_fusion.1 = f32[64,128]{1,0:T(8,128)S(1)} fusion(bf16[64,128,128]{2,1,0:T(8,128)(2,1)} %copy-done.1), kind=kLoop, calls=%fused_computation.22 | loop fusion | flops 2088960 | bytes 2129920 | tf_op jit(solution)/shard_map/while/body/eval_jaxpr/reduce_sum | solution.py:57
  76.5 1.7 %convert_reduce_fusion = f32[64,192]{0,1:T(8,128)S(1)} fusion(bf16[64,192,128]{2,0,1:T(8,128)(2,1)S(1)} %copy-done), kind=kLoop, calls=%fused_computation.18 | loop fusion | flops 3133440 | bytes 3194880 | tf_op jit(solution)/shard_map/while/body/eval_jaxpr/reduce_sum | solution.py:56
  78.1 1.3 convolution_bitcast_fusion
  79.5 18.1 %reduce-scatter.3.cloned.1.call-done = f32[1,192,128]{2,1,0:T(8,128)} async-done(((f32[4,192,128]{2,1,0:T(8,128)}), f32[1,192,128]{2,1,0:T(8,128)}) %reduce-scatter.3.cloned.1.call-update) | async-done | bytes 98320 | tf_op jit(solution)/shard_map/reduce_scatter | solution.py:93
  97.6 21.3 %reduce-scatter.5.cloned.1.call-done = f32[1,192,128]{2,1,0:T(8,128)} async-done(((f32[4,192,128]{2,1,0:T(8,128)}), f32[1,192,128]{2,1,0:T(8,128)}) %reduce-scatter.5.cloned.1.call-update) | async-done | bytes 98320 | tf_op jit(solution)/shard_map/reduce_scatter | solution.py:94
  119.0 18.7 %all-reduce.8.cloned.1.call-done = (f32[1,192,128]{2,1,0:T(8,128)}, f32[1,192,128]{2,1,0:T(8,128)}) async-done(((f32[1,192,128]{2,1,0:T(8,128)}, f32[1,192,128]{2,1,0:T(8,128)}), (f32[1,192,128]{2,1,0:T(8,128)}, f32[1,192,128]{2,1,0:T(8,128)})) %all-reduce.8.cloned.1.call-update) | async-done | bytes 196624 | tf_op jit(solution)/shard_map/psum | solution.py:96
  137.7 0.9 constant_dynamic-update-slice_fusion.1
  138.6 0.9 constant_dynamic-update-slice_fusion
  139.5 3.7 %collective-permute-start = (f32[2,32,128]{2,1,0:T(8,128)S(1)}, f32[2,32,128]{2,1,0:T(8,128)S(1)}, u32[]{:S(2)}, u32[]{:S(2)}) collective-permute-start(f32[2,32,128]{2,1,0:T(8,128)S(1)} %get-tuple-element.70), channel_id=1, source_target_pairs={{0,2},{1,3},{4,6},{5,7},{8,10},{9,11},{12,14},{13,15},{16,18},{17,... | collective-permute-start | bytes 98312 | tf_op jit(solution)/shard_map/ppermute | solution.py:19
  143.3 1.3 collective-permute-start.1
  144.8 4.2 %collective-permute-done.1 = f32[2,32,128]{2,1,0:T(8,128)S(1)} collective-permute-done((f32[2,32,128]{2,1,0:T(8,128)S(1)}, f32[2,32,128]{2,1,0:T(8,128)S(1)}, u32[]{:S(2)}, u32[]{:S(2)}) %collective-permute-start.1) | collective-permute-done | bytes 32800 | tf_op jit(solution)/shard_map/ppermute | solution.py:20
  (26 shorter events, 2.7 us)
Async XLA Ops:
  7.2 90.5 %reduce-scatter.3.cloned.1.call-start = ((), (), s32[]{:S(2)}) async-start(), calls=%async_computation.2 | async-start | bytes 491520 | tf_op jit(solution)/shard_map/reduce_scatter | solution.py:93
  11.6 21.0 %copy-start.1 = (bf16[64,128,128]{2,1,0:T(8,128)(2,1)}, bf16[64,128,128]{2,1,0:T(8,128)(2,1)S(1)}, u32[]{:S(2)}) copy-start(bf16[64,128,128]{2,1,0:T(8,128)(2,1)S(1)} %gather_fusion.3) | copy-start | bytes 6291460
  58.1 8.5 %copy-start.2 = (f32[64]{0:T(128)S(1)}, f32[64]{0:T(128)}, u32[]{:S(2)}) copy-start(f32[64]{0:T(128)} %param.15) | copy-start | bytes 772
  58.1 8.5 %copy-start.3 = (s32[64,1]{0,1:T(1,128)S(1)}, s32[64,1]{0,1:T(1,128)}, u32[]{:S(2)}) copy-start(s32[64,1]{0,1:T(1,128)} %param.12) | copy-start | bytes 772
  66.6 9.8 %copy-start = (bf16[64,192,128]{2,0,1:T(8,128)(2,1)S(1)}, bf16[64,192,128]{2,0,1:T(8,128)(2,1)}, u32[]{:S(2)}) copy-start(bf16[64,192,128]{2,0,1:T(8,128)(2,1)} %gather_fusion.2) | copy-start | bytes 9437188
  73.9 45.0 %reduce-scatter.5.cloned.1.call-start = ((), (), s32[]{:S(2)}) async-start(), calls=%async_computation.3 | async-start | bytes 491520 | tf_op jit(solution)/shard_map/reduce_scatter | solution.py:94
  79.5 58.3 %all-reduce.8.cloned.1.call-start = ((), (), s32[]{:S(2)}) async-start(), calls=%async_computation.4 | async-start | bytes 393216 | tf_op jit(solution)/shard_map/psum | solution.py:96
  139.5 5.3 %collective-permute-start = (f32[2,32,128]{2,1,0:T(8,128)S(1)}, f32[2,32,128]{2,1,0:T(8,128)S(1)}, u32[]{:S(2)}, u32[]{:S(2)}) collective-permute-start(f32[2,32,128]{2,1,0:T(8,128)S(1)} %get-tuple-element.70), channel_id=1, source_target_pairs={{0,2},{1,3},{4,6},{5,7},{8,10},{9,11},{12,14},{13,15},{16,18},{17,... | collective-permute-start | bytes 98312 | tf_op jit(solution)/shard_map/ppermute | solution.py:19
  143.3 5.8 %collective-permute-start.1 = (f32[2,32,128]{2,1,0:T(8,128)S(1)}, f32[2,32,128]{2,1,0:T(8,128)S(1)}, u32[]{:S(2)}, u32[]{:S(2)}) collective-permute-start(f32[2,32,128]{2,1,0:T(8,128)S(1)} %get-tuple-element.69), channel_id=1, source_target_pairs={{2,0},{3,1},{6,4},{7,5},{10,8},{11,9},{14,12},{15,13},{18,16},{19,... | collective-permute-start | bytes 98312 | tf_op jit(solution)/shard_map/ppermute | solution.py:20
Sparse Core Ops, SparseCore 0:
  74.1 23.5 reduce-scatter.2
  99.9 19.0 reduce-scatter.4
  121.3 16.3 all-reduce.7
where the time goes:
time: 157 us; the launch traced here: 156 us
  waiting for transfers between devices  62.8 us (40%)
  other arithmetic  29.9 us (19%)
  local copies, waits for them, and re-layouts  26.6 us (17%)
  matrix products  17.8 us (11%)
  between operations  13.9 us (9%)
  starting transfers between devices  5.31 us (3%)
    reduce_scatter x1, waiting for transfers between devices, on_device(): lax.psum_scatter(den_sum, 'ra', scatter_dimension=0, tiled=True)  21.3 us
    psum x1, waiting for transfers between devices, on_device(): num_sum, den_sum = lax.psum((num_sum[0], den_sum[0]), 'rep')  18.7 us
    reduce_scatter x1, waiting for transfers between devices, on_device(): lax.psum_scatter(num_sum, 'ra', scatter_dimension=0, tiled=True)  18.1 us
    add x1, other arithmetic, convolve(): along = along + row_taps[:, k][:, None, None] * padded[:, k:k + height, :]  15.5 us
    gather x1, local copies, waits for them, and re-layouts, place(): lax.dynamic_slice(row_pad, (v, start, jnp.int32(0)), (1, canvas_rows, PIX))  14.4 us
    dot_general x1, matrix products, render(): jnp.einsum('nia,nak->nik', rows, mid, preferred_element_type=jnp.float32)  10 us
    add x1, other arithmetic, convolve(): result = result + col_taps[:, k][:, None, None] * padded[:, :, k:k + width]  8.48 us
    dot_general x1, matrix products, step(): jnp.einsum('tg,tik->gik', shares, matched, precision=lax.Precision.HIGHEST)  6.47 us
  transfers between devices with their start and end apart: 5, of which 5 were waited for; matrix products, arithmetic and copies ran while one was open for 3% of the time, Pallas kernels for 0%

commit v1 on v0

v1 whole, which is shorter than its diff:
```python
import functools

import jax
import jax.numpy as jnp
from jax import lax
from jax.experimental import pallas as pl
from jax.experimental.pallas import tpu as pltpu
from jax.sharding import PartitionSpec as P

PIX = 128
MARGIN = 32
ROWS = PIX + 2 * MARGIN
TAPS = 5
EDGE = TAPS // 2
CHUNK = 16
SPAN = PIX + 8
WIDE = 2 * PIX
LINK = jnp.float32
MESH = pl.DeviceIdType.MESH
VMEM = pl.BlockSpec(memory_space=pltpu.VMEM)
SMEM = pl.BlockSpec(memory_space=pltpu.SMEM)
ANY = pl.BlockSpec(memory_space=pl.ANY)


def in_two(value):
    high = value.astype(jnp.bfloat16)
    return high, (value - high.astype(jnp.float32)).astype(jnp.bfloat16)


def local_kernel(
    bands, visits, tiles_hbm, route, visit, offset, weight, taps, maps,
    num_out, den_out, cols_out,
    raw, spread, mid, row_maps, col_maps, pad, row_sums, canvas, den, sems,
):
    count = tiles_hbm.shape[0]
    chunks = count // CHUNK

    def fetch(c):
        return pltpu.make_async_copy(
            tiles_hbm.at[pl.ds(c * CHUNK, CHUNK)], raw.at[c], sems.at[c]
        )

    for c in range(chunks):
        fetch(c).start()

    pad[...] = jnp.zeros_like(pad)
    canvas[...] = jnp.zeros_like(canvas)
    den[...] = jnp.zeros_like(den)
    ones = jnp.ones((8, PIX), jnp.bfloat16)
    over = (((1,), (1,)), ((), ()))

    def prepare(v, _):
        pad[0, 8 : 8 + PIX, :] = maps[v, 0].astype(jnp.float32)
        pad[1, 8 : 8 + PIX, :] = maps[v, 1].astype(jnp.float32)
        rows = jnp.zeros((SPAN, PIX), jnp.float32)
        cols = jnp.zeros((PIX, PIX), jnp.float32)
        for k in range(TAPS):
            rows += taps[k, 0, v] * pad[0, 8 + k - 2 * EDGE : 8 + k - 2 * EDGE + SPAN, :]
            cols += taps[k, 1, v] * pad[1, 8 + k - EDGE : 8 + k - EDGE + PIX, :]
        high, low = in_two(rows)
        row_maps[v, :SPAN, :PIX] = high
        row_maps[v, :SPAN, PIX : 2 * PIX] = low
        row_maps[v, :SPAN, 2 * PIX :] = high
        col_maps[v, :, :PIX], col_maps[v, :, PIX:] = in_two(cols.T)
        sums = lax.dot_general(ones, maps[v, 0], over, preferred_element_type=jnp.float32)
        row_sums[pl.ds(v, 1), :] = sums[:1]
        sums = lax.dot_general(ones, maps[v, 1], over, preferred_element_type=jnp.float32)
        cols_out[pl.ds(v, 1), :] = sums[:1]
        return 0

    lax.fori_loop(0, visits, prepare, 0)

    def work(c, _):
        fetch(c).wait()
        for a in range(PIX):
            spread[a * CHUNK : (a + 1) * CHUNK, :] = raw[c, :, a * PIX : (a + 1) * PIX].astype(
                jnp.float32
            )
        for j in range(CHUNK):
            t = c * CHUNK + j
            grid = spread[pl.ds(j, PIX, stride=CHUNK), :].astype(jnp.bfloat16)
            part = jnp.dot(grid, col_maps[visit[t]], preferred_element_type=jnp.float32)
            high, low = in_two(weight[t] * (part[:, :PIX] + part[:, PIX:]))
            mid[j, :PIX, :] = high
            mid[j, PIX : 2 * PIX, :] = high
            mid[j, 2 * PIX :, :] = low
        for j in range(CHUNK):
            t = c * CHUNK + j
            image = jnp.dot(row_maps[visit[t]], mid[j], preferred_element_type=jnp.float32)
            canvas[route[t], pl.ds(offset[t], SPAN), :] += image[:SPAN]
            line = weight[t] * row_sums[pl.ds(visit[t], 1), :]
            line = pltpu.roll(jnp.concatenate([line, jnp.zeros_like(line)], axis=1), offset[t], 1)
            at = pl.ds(route[t] * visits + visit[t], 1)
            den[0, at, :] += line[:, :PIX]
            den[1, at, :] += line[:, PIX:]
        return 0

    lax.fori_loop(0, chunks, work, 0)
    for g in range(bands):
        num_out[g] = canvas[g, EDGE : EDGE + ROWS, :].astype(num_out.dtype)
    for side in range(2):
        den_out[:, side * PIX : (side + 1) * PIX] = den[side]


def reduce_kernel(
    bands, decs, visits, num_in, den_in, cols, folded, weight_map,
    part, den_part, total, den_total, main, strip, den_strip,
    send, recv, send_den, recv_den, own, send_two, recv_two,
):
    z, x, h = lax.axis_index("ra"), lax.axis_index("dec"), lax.axis_index("rep")
    half = ROWS // 2
    barrier = pltpu.get_barrier_semaphore()
    others = [(j, k) for j in range(bands - 1, -1, -1) for k in range(2) if (j, k) != (0, 0)]

    def peer(j, k):
        return lax.rem(z + j, bands), lax.rem(h + k, 2)

    for j, k in others:
        to, core = peer(j, k)
        pl.semaphore_signal(
            barrier, inc=1, device_id={"ra": to, "rep": core}, device_id_type=MESH
        )
    for cond, to in ((x > 0, x - 1), (x < decs - 1, x + 1)):
        @pl.when(cond)
        def _():
            for core in range(2):
                pl.semaphore_signal(
                    barrier, inc=1, device_id={"dec": to, "rep": core}, device_id_type=MESH
                )
    beside = jnp.where(x > 0, 2, 0) + jnp.where(x < decs - 1, 2, 0)
    pl.semaphore_wait(barrier, len(others) + beside)

    copies = {}
    for j, k in others:
        to, core = peer(j, k)
        s = j * 2 + k
        where = {"ra": to, "rep": core}
        rows = pl.ds(pl.multiple_of(core * half, half), half)
        copies[s] = (
            pltpu.make_async_remote_copy(
                num_in.at[to, rows], part.at[s], send.at[s], recv.at[s],
                device_id=where, device_id_type=MESH,
            ),
            pltpu.make_async_remote_copy(
                den_in.at[pl.ds(pl.multiple_of(to * visits, visits), visits)],
                den_part.at[s], send_den.at[s], recv_den.at[s],
                device_id=where, device_id_type=MESH,
            ),
        )
        for copy in copies[s]:
            copy.start()
    rows = pl.ds(pl.multiple_of(h * half, half), half)
    mine = (
        pltpu.make_async_copy(num_in.at[z, rows], part.at[0], own.at[0]),
        pltpu.make_async_copy(
            den_in.at[pl.ds(pl.multiple_of(z * visits, visits), visits)], den_part.at[0], own.at[1]
        ),
    )
    for copy in mine:
        copy.start()
    for slot, cond in ((0, x == decs - 1), (1, x == 0)):
        @pl.when(cond)
        def _():
            strip[slot] = jnp.zeros(strip.shape[1:], strip.dtype)
            den_strip[slot] = jnp.zeros(den_strip.shape[1:], den_strip.dtype)

    for copy in mine:
        copy.wait()
    acc = part[0].astype(jnp.float32)
    den_acc = den_part[0]
    for s in range(1, 2 * bands):
        for copy in copies[s]:
            copy.wait_recv()
        acc += part[s].astype(jnp.float32)
        den_acc += den_part[s]
    total[...] = acc
    den_total[...] = den_acc

    own_rows = pl.ds(pl.multiple_of(MARGIN * (1 - h), MARGIN), PIX // 2)
    strip_rows = pl.ds(pl.multiple_of((PIX // 2) * h, MARGIN), MARGIN)
    across = pltpu.make_async_remote_copy(
        total.at[own_rows], main, send_two.at[4], recv_two.at[4],
        device_id={"rep": 1 - h}, device_id_type=MESH,
    )

    def to_next(core, slot, target):
        where = {"dec": target, "rep": core}
        return (
            pltpu.make_async_remote_copy(
                total.at[strip_rows], strip.at[slot], send_two.at[2 * core],
                recv_two.at[2 * slot], device_id=where, device_id_type=MESH,
            ),
            pltpu.make_async_remote_copy(
                den_total, den_strip.at[slot], send_two.at[2 * core + 1],
                recv_two.at[2 * slot + 1], device_id=where, device_id_type=MESH,
            ),
        )

    sides = ((0, (h == 0) & (x > 0), x - 1), (1, (h == 1) & (x < decs - 1), x + 1))
    for slot, cond, target in sides:
        @pl.when(cond)
        def _():
            for core in range(2):
                for copy in to_next(core, slot, target):
                    copy.start()
    across.start()

    def spread_out(lines):
        return lax.dot_general(
            lines, cols[...], (((0,), (0,)), ((), ())),
            precision=lax.Precision.HIGHEST, preferred_element_type=jnp.float32,
        )

    whole = spread_out(den_total[...])[MARGIN : MARGIN + PIX]
    folded[pl.ds(pl.multiple_of((PIX // 2) * h, MARGIN), PIX // 2), :] = total[own_rows, :]
    for slot, cond in ((0, x < decs - 1), (1, x > 0)):
        @pl.when(cond)
        def _():
            for copy in to_next(0, slot, x):
                copy.wait_recv()
    after = spread_out(den_strip[0, :, :PIX])[:MARGIN]
    before = spread_out(den_strip[1, :, PIX:])[ROWS - MARGIN - PIX : ROWS - PIX]
    across.wait_recv()
    folded[pl.ds(pl.multiple_of((PIX // 2) * (1 - h), MARGIN), PIX // 2), :] = main[...]
    low, high = PIX - MARGIN, MARGIN
    top = whole[:high] + before
    bottom = whole[low:] + after
    weight_map[:high, :] = top
    weight_map[high:low, :] = whole[high:low]
    weight_map[low:, :] = bottom
    folded[:high, :] += strip[1]
    folded[low:, :] += strip[0]

    for s in range(1, 2 * bands):
        for copy in copies[s]:
            copy.wait_send()
    across.wait_send()
    for slot, cond, target in sides:
        @pl.when(cond)
        def _():
            for core in range(2):
                for copy in to_next(core, slot, target):
                    copy.wait_send()


def divide_kernel(num, den, coadd, weight_map):
    coadd[...] = num[...] / (den[...] + 1.0)
    weight_map[...] = den[...]


def on_device(bands, decs, tiles, route, visit, offset, weight, maps, taps):
    count = tiles.shape[0]
    visits = maps.shape[0]
    half = ROWS // 2
    f32, bf16 = jnp.float32, jnp.bfloat16
    num, den, cols = pl.pallas_call(
        functools.partial(local_kernel, bands, visits),
        out_shape=(
            jax.ShapeDtypeStruct((bands, ROWS, PIX), LINK),
            jax.ShapeDtypeStruct((bands * visits, WIDE), f32),
            jax.ShapeDtypeStruct((visits, PIX), f32),
        ),
        in_specs=[ANY, SMEM, SMEM, SMEM, SMEM, SMEM, VMEM],
        out_specs=(VMEM, VMEM, VMEM),
        scratch_shapes=[
            pltpu.VMEM((count // CHUNK, CHUNK, PIX * PIX), bf16),
            pltpu.VMEM((PIX * CHUNK, PIX), f32),
            pltpu.VMEM((CHUNK, 3 * PIX, PIX), bf16),
            pltpu.VMEM((visits, SPAN + 8, 3 * PIX), bf16),
            pltpu.VMEM((visits, PIX, 2 * PIX), bf16),
            pltpu.VMEM((2, PIX + 24, PIX), f32),
            pltpu.VMEM((visits, PIX), f32),
            pltpu.VMEM((bands, 2 * MARGIN + SPAN, PIX), f32),
            pltpu.VMEM((2, bands * visits, PIX), f32),
            pltpu.SemaphoreType.DMA((count // CHUNK,)),
        ],
        name="local_sums",
    )(
        tiles, route.reshape(count), visit, offset, weight,
        taps.transpose(2, 1, 0), maps,
    )
    dma = pltpu.SemaphoreType.DMA
    cell = jax.ShapeDtypeStruct((PIX, PIX), f32)
    folded = pl.pallas_call(
        functools.partial(reduce_kernel, bands, decs, visits),
        out_shape=(cell, cell),
        in_specs=[ANY, ANY, VMEM],
        out_specs=(VMEM, VMEM),
        scratch_shapes=[
            pltpu.VMEM((2 * bands, half, PIX), LINK),
            pltpu.VMEM((2 * bands, visits, WIDE), f32),
            pltpu.VMEM((half, PIX), f32),
            pltpu.VMEM((visits, WIDE), f32),
            pltpu.VMEM((PIX // 2, PIX), f32),
            pltpu.VMEM((2, MARGIN, PIX), f32),
            pltpu.VMEM((2, visits, WIDE), f32),
            dma((2 * bands,)),
            dma((2 * bands,)),
            dma((2 * bands,)),
            dma((2 * bands,)),
            dma((2,)),
            dma((5,)),
            dma((5,)),
        ],
        compiler_params=pltpu.CompilerParams(collective_id=0, has_side_effects=True),
        name="reduce_cells",
    )(num, den, cols)
    return pl.pallas_call(
        divide_kernel,
        out_shape=(cell, cell),
        in_specs=[VMEM, VMEM],
        out_specs=(VMEM, VMEM),
        name="divide_cells",
    )(*folded)


def solution(mesh):
    spread = ("groups", "ra", "dec", "rep")
    in_specs = (
        P(spread, None),
        P(spread, None),
        P(spread),
        P(spread),
        P(spread),
        P("groups", None, None, None),
        P("groups", None, None),
    )
    out_specs = (P(("groups", "dec"), "ra"), P(("groups", "dec"), "ra"))
    return jax.shard_map(
        functools.partial(on_device, mesh.shape["ra"], mesh.shape["dec"]),
        mesh=mesh, in_specs=in_specs, out_specs=out_specs, check_vma=False,
    )
```

time: 157 us -> 32.2 us (0.21)
  waiting for transfers between devices: 62.8 us -> 0 us
  Pallas kernels: 0 us -> 31.2 us
  other arithmetic: 29.9 us -> 0 us
  local copies, waits for them, and re-layouts: 26.6 us -> 0 us
  matrix products: 17.8 us -> 0 us
  between operations: 13.9 us -> 0.65 us
  starting transfers between devices: 5.31 us -> 0 us
    reduce_scatter x2 -> x0, waiting for transfers between devices: 39.5 us -> none  [the longest x1 21.3 us: on_device(): lax.psum_scatter(den_sum, 'ra', scatter_dimension=0, tiled=True)]
    pallas_call x0 -> x3, Pallas kernels: none -> 31.2 us  [the longest x1 21.6 us: on_device(): pl.pallas_call(functools.partial(reduce_kernel, bands, decs, visits), out...]
    add x2 -> x0, other arithmetic: 24 us -> none  [the longest x1 15.5 us: convolve(): along = along + row_taps[:, k][:, None, None] * padded[:, k:k + height, :]]
    psum x1 -> x0, waiting for transfers between devices: 18.7 us -> none  [on_device(): num_sum, den_sum = lax.psum((num_sum[0], den_sum[0]), 'rep')]
    gather x4 -> x0, local copies, waits for them, and re-layouts: 18 us -> none  [the longest x1 14.4 us: place(): lax.dynamic_slice(row_pad, (v, start, jnp.int32(0)), (1, canvas_rows, PIX))]
    dot_general x3 -> x0, matrix products: 17.8 us -> none  [the longest x1 10 us: render(): jnp.einsum('nia,nak->nik', rows, mid, preferred_element_type=jnp.float32)]
    unnamed x12 -> x0, local copies, waits for them, and re-layouts: 5.47 us -> none
    ppermute x2 -> x0, starting transfers between devices: 4.97 us -> none  [the longest x1 3.68 us: padded_2(): before = lax.ppermute(last, axis, up)]
  transfers between devices with their start and end apart: 5 -> 0, of which waited for: 5 -> 0; matrix products, arithmetic and copies ran while one was open for 3% -> 0% of each run, Pallas kernels for 0% -> 0%
where the time goes in v1:
time: 32.2 us; the launch traced here: 31.9 us
  Pallas kernels  31.2 us (97%)
  between operations  0.65 us (2%)
    pallas_call x1, Pallas kernels, on_device(): pl.pallas_call(functools.partial(reduce_kernel, bands, decs, visits), out...  21.6 us
    pallas_call x1, Pallas kernels, on_device(): pl.pallas_call(functools.partial(local_kernel, bands, visits), out_shape=...  8.15 us
    pallas_call x1, Pallas kernels, on_device(): pl.pallas_call(divide_kernel, out_shape=(cell, cell), in_specs=[VMEM, VME...  1.53 us

profile of v1, /device:TPU:0, one launch (start us, length us, event | category | flops | bytes accessed | tf_op | source)
XLA Modules:
  0.0 31.9 jit_solution(13604999112599116883)
XLA Ops:
  0.6 8.2 %local_sums.1 = (f32[4,192,128]{2,1,0:T(8,128)}, f32[32,256]{1,0:T(8,128)}, f32[8,128]{1,0:T(8,128)}) custom-call(bf16[64,16384]{1,0:T(8,128)(2,1)} %tiles_hbm.1, s32[64]{0:T(128)} %bitcast.3, s32[64]{0:T(128)} %visit.1, s32[64]{0:T(128)} %offset.1, f32[64]{0:T(128)} %weight.1, f32[5,2,8]{2,1,0:T(2,128)} %bitcast.2, bf16[8,2,128,128]{3,2,1,0:T(8,128)(2,1)} %maps.1), custom_call_target="tpu_custom_call" | custom-call | tf_op jit(solution)/shard_map/local_sums/pallas_call | solution.py:256
  8.8 21.6 %reduce_cells.1 = (f32[128,128]{1,0:T(8,128)}, f32[128,128]{1,0:T(8,128)}) custom-call(f32[4,192,128]{2,1,0:T(8,128)} %get-tuple-element.7.num_in, f32[32,256]{1,0:T(8,128)} %get-tuple-element.8.den_in, f32[8,128]{1,0:T(8,128)} %get-tuple-element.9.cols), custom_call_target="tpu_custom_call" | custom-call | tf_op jit(solution)/shard_map/reduce_cells/pallas_call | solution.py:284
  30.4 1.5 %divide_cells.1 = (f32[128,128]{1,0:T(8,128)}, f32[128,128]{1,0:T(8,128)}) custom-call(f32[128,128]{1,0:T(8,128)} %get-tuple-element.10.num, f32[128,128]{1,0:T(8,128)} %get-tuple-element.11.den), custom_call_target="tpu_custom_call" | custom-call | tf_op jit(solution)/shard_map/divide_cells/pallas_call | solution.py:308

commit v2 on v1

--- a/solution.py
+++ b/solution.py
@@ -15,7 +15,6 @@
 CHUNK = 16
 SPAN = PIX + 8
 WIDE = 2 * PIX
-LINK = jnp.float32
 MESH = pl.DeviceIdType.MESH
 VMEM = pl.BlockSpec(memory_space=pltpu.VMEM)
 SMEM = pl.BlockSpec(memory_space=pltpu.SMEM)
@@ -104,22 +103,29 @@
 
 def reduce_kernel(
     bands, decs, visits, num_in, den_in, cols, folded, weight_map,
-    part, den_part, total, den_total, main, strip, den_strip,
-    send, recv, send_den, recv_den, own, send_two, recv_two,
+    kept, pair, sums, part, den_kept, den_pair, den_sums, den_part, total, den_total,
+    main, strip, den_strip,
+    own, send_pair, recv_pair, send, recv, send_den, recv_den, send_two, recv_two,
 ):
     z, x, h = lax.axis_index("ra"), lax.axis_index("dec"), lax.axis_index("rep")
     half = ROWS // 2
+    order = sorted(range(1, bands), key=lambda j: -min(j, bands - j)) + [0]
+
+    def band(j):
+        return lax.rem(z + j, bands)
+
+    def half_of(j, core):
+        return num_in.at[band(j), pl.ds(pl.multiple_of(core * half, half), half)]
+
+    mine = [pltpu.make_async_copy(half_of(j, h), kept.at[j], own.at[j]) for j in range(bands)]
+    mine.append(pltpu.make_async_copy(den_in, den_kept, own.at[bands]))
+    for copy in mine:
+        copy.start()
+
     barrier = pltpu.get_barrier_semaphore()
-    others = [(j, k) for j in range(bands - 1, -1, -1) for k in range(2) if (j, k) != (0, 0)]
-
-    def peer(j, k):
-        return lax.rem(z + j, bands), lax.rem(h + k, 2)
-
-    for j, k in others:
-        to, core = peer(j, k)
-        pl.semaphore_signal(
-            barrier, inc=1, device_id={"ra": to, "rep": core}, device_id_type=MESH
-        )
+    peers = [{"rep": 1 - h}] + [{"ra": band(j)} for j in range(1, bands)]
+    for peer in peers:
+        pl.semaphore_signal(barrier, inc=1, device_id=peer, device_id_type=MESH)
     for cond, to in ((x > 0, x - 1), (x < decs - 1, x + 1)):
         @pl.when(cond)
         def _():
@@ -128,51 +134,62 @@
                     barrier, inc=1, device_id={"dec": to, "rep": core}, device_id_type=MESH
                 )
     beside = jnp.where(x > 0, 2, 0) + jnp.where(x < decs - 1, 2, 0)
-    pl.semaphore_wait(barrier, len(others) + beside)
+    pl.semaphore_wait(barrier, len(peers) + beside)
+
+    pairs = {
+        j: pltpu.make_async_remote_copy(
+            half_of(j, 1 - h), pair.at[j], send_pair.at[j], recv_pair.at[j],
+            device_id={"rep": 1 - h}, device_id_type=MESH,
+        )
+        for j in order
+    }
+    den_copy = pltpu.make_async_remote_copy(
+        den_in, den_pair, send_pair.at[bands], recv_pair.at[bands],
+        device_id={"rep": 1 - h}, device_id_type=MESH,
+    )
+    for n, j in enumerate(order):
+        pairs[j].start()
+        if n == 0:
+            den_copy.start()
+    for slot, cond in ((0, x == decs - 1), (1, x == 0)):
+        @pl.when(cond)
+        def _():
+            strip[slot] = jnp.zeros(strip.shape[1:], strip.dtype)
+            den_strip[slot] = jnp.zeros(den_strip.shape[1:], den_strip.dtype)
 
     copies = {}
-    for j, k in others:
-        to, core = peer(j, k)
-        s = j * 2 + k
-        where = {"ra": to, "rep": core}
-        rows = pl.ds(pl.multiple_of(core * half, half), half)
-        copies[s] = (
+    for n, j in enumerate(order):
+        mine[j].wait()
+        pairs[j].wait_recv()
+        sums[j] = kept[j] + pair[j]
+        if n == 0:
+            mine[bands].wait()
+            den_copy.wait_recv()
+            den_sums[...] = den_kept[...] + den_pair[...]
+        if j == 0:
+            continue
+        lines = pl.ds(pl.multiple_of(band(j) * visits, visits), visits)
+        where = {"ra": band(j)}
+        copies[j] = (
             pltpu.make_async_remote_copy(
-                num_in.at[to, rows], part.at[s], send.at[s], recv.at[s],
+                sums.at[j], part.at[j], send.at[j], recv.at[j],
                 device_id=where, device_id_type=MESH,
             ),
             pltpu.make_async_remote_copy(
-                den_in.at[pl.ds(pl.multiple_of(to * visits, visits), visits)],
-                den_part.at[s], send_den.at[s], recv_den.at[s],
+                den_sums.at[lines], den_part.at[j], send_den.at[j], recv_den.at[j],
                 device_id=where, device_id_type=MESH,
             ),
         )
-        for copy in copies[s]:
+        for copy in copies[j]:
             copy.start()
-    rows = pl.ds(pl.multiple_of(h * half, half), half)
-    mine = (
-        pltpu.make_async_copy(num_in.at[z, rows], part.at[0], own.at[0]),
-        pltpu.make_async_copy(
-            den_in.at[pl.ds(pl.multiple_of(z * visits, visits), visits)], den_part.at[0], own.at[1]
-        ),
-    )
-    for copy in mine:
-        copy.start()
-    for slot, cond in ((0, x == decs - 1), (1, x == 0)):
-        @pl.when(cond)
-        def _():
-            strip[slot] = jnp.zeros(strip.shape[1:], strip.dtype)
-            den_strip[slot] = jnp.zeros(den_strip.shape[1:], den_strip.dtype)
-
-    for copy in mine:
-        copy.wait()
-    acc = part[0].astype(jnp.float32)
-    den_acc = den_part[0]
-    for s in range(1, 2 * bands):
-        for copy in copies[s]:
+
+    acc = sums[0]
+    den_acc = den_sums[pl.ds(pl.multiple_of(z * visits, visits), visits), :]
+    for j in reversed(order[:-1]):
+        for copy in copies[j]:
             copy.wait_recv()
-        acc += part[s].astype(jnp.float32)
-        den_acc += den_part[s]
+        acc += part[j]
+        den_acc += den_part[j]
     total[...] = acc
     den_total[...] = den_acc
 
@@ -231,8 +248,11 @@
     folded[:high, :] += strip[1]
     folded[low:, :] += strip[0]
 
-    for s in range(1, 2 * bands):
-        for copy in copies[s]:
+    for j in order:
+        pairs[j].wait_send()
+    den_copy.wait_send()
+    for j in order[:-1]:
+        for copy in copies[j]:
             copy.wait_send()
     across.wait_send()
     for slot, cond, target in sides:
@@ -256,7 +276,7 @@
     num, den, cols = pl.pallas_call(
         functools.partial(local_kernel, bands, visits),
         out_shape=(
-            jax.ShapeDtypeStruct((bands, ROWS, PIX), LINK),
+            jax.ShapeDtypeStruct((bands, ROWS, PIX), f32),
             jax.ShapeDtypeStruct((bands * visits, WIDE), f32),
             jax.ShapeDtypeStruct((visits, PIX), f32),
         ),
@@ -287,18 +307,26 @@
         in_specs=[ANY, ANY, VMEM],
         out_specs=(VMEM, VMEM),
         scratch_shapes=[
-            pltpu.VMEM((2 * bands, half, PIX), LINK),
-            pltpu.VMEM((2 * bands, visits, WIDE), f32),
+            pltpu.VMEM((bands, half, PIX), f32),
+            pltpu.VMEM((bands, half, PIX), f32),
+            pltpu.VMEM((bands, half, PIX), f32),
+            pltpu.VMEM((bands, half, PIX), f32),
+            pltpu.VMEM((bands * visits, WIDE), f32),
+            pltpu.VMEM((bands * visits, WIDE), f32),
+            pltpu.VMEM((bands * visits, WIDE), f32),
+            pltpu.VMEM((bands, visits, WIDE), f32),
             pltpu.VMEM((half, PIX), f32),
             pltpu.VMEM((visits, WIDE), f32),
             pltpu.VMEM((PIX // 2, PIX), f32),
             pltpu.VMEM((2, MARGIN, PIX), f32),
             pltpu.VMEM((2, visits, WIDE), f32),
-            dma((2 * bands,)),
-            dma((2 * bands,)),
-            dma((2 * bands,)),
-            dma((2 * bands,)),
-            dma((2,)),
+            dma((bands + 1,)),
+            dma((bands + 1,)),
+            dma((bands + 1,)),
+            dma((bands,)),
+            dma((bands,)),
+            dma((bands,)),
+            dma((bands,)),
             dma((5,)),
             dma((5,)),
         ],

time: 32.2 us -> 27.2 us (0.84)
  Pallas kernels: 31.2 us -> 26.3 us
    pallas_call x1, Pallas kernels: 21.6 us -> 16.6 us  [on_device(): pl.pallas_call(functools.partial(reduce_kernel, bands, decs, visits), out...]
where the time goes in v2:
time: 27.2 us; the launch traced here: 26.9 us
  Pallas kernels  26.3 us (97%)
  between operations  0.65 us (2%)
    pallas_call x1, Pallas kernels, on_device(): pl.pallas_call(functools.partial(reduce_kernel, bands, decs, visits), out...  16.6 us
    pallas_call x1, Pallas kernels, on_device(): pl.pallas_call(functools.partial(local_kernel, bands, visits), out_shape=...  8.15 us
    pallas_call x1, Pallas kernels, on_device(): pl.pallas_call(divide_kernel, out_shape=(cell, cell), in_specs=[VMEM, VME...  1.53 us

profile of v2, /device:TPU:0, one launch (start us, length us, event | category | flops | bytes accessed | tf_op | source)
XLA Modules:
  0.0 26.9 jit_solution(17813306784893176585)
XLA Ops:
  0.6 8.1 %local_sums.1 = (f32[4,192,128]{2,1,0:T(8,128)}, f32[32,256]{1,0:T(8,128)}, f32[8,128]{1,0:T(8,128)}) custom-call(bf16[64,16384]{1,0:T(8,128)(2,1)} %tiles_hbm.1, s32[64]{0:T(128)} %bitcast.3, s32[64]{0:T(128)} %visit.1, s32[64]{0:T(128)} %offset.1, f32[64]{0:T(128)} %weight.1, f32[5,2,8]{2,1,0:T(2,128)} %bitcast.2, bf16[8,2,128,128]{3,2,1,0:T(8,128)(2,1)} %maps.1), custom_call_target="tpu_custom_call" | custom-call | tf_op jit(solution)/shard_map/local_sums/pallas_call | solution.py:276
  8.8 16.6 %reduce_cells.1 = (f32[128,128]{1,0:T(8,128)}, f32[128,128]{1,0:T(8,128)}) custom-call(f32[4,192,128]{2,1,0:T(8,128)} %get-tuple-element.7.num_in, f32[32,256]{1,0:T(8,128)} %get-tuple-element.8.den_in, f32[8,128]{1,0:T(8,128)} %get-tuple-element.9.cols), custom_call_target="tpu_custom_call" | custom-call | tf_op jit(solution)/shard_map/reduce_cells/pallas_call | solution.py:304
  25.4 1.5 %divide_cells.1 = (f32[128,128]{1,0:T(8,128)}, f32[128,128]{1,0:T(8,128)}) custom-call(f32[128,128]{1,0:T(8,128)} %get-tuple-element.10.num, f32[128,128]{1,0:T(8,128)} %get-tuple-element.11.den), custom_call_target="tpu_custom_call" | custom-call | tf_op jit(solution)/shard_map/divide_cells/pallas_call | solution.py:336

commit v3 on v2

--- a/solution.py
+++ b/solution.py
@@ -13,6 +13,7 @@
 TAPS = 5
 EDGE = TAPS // 2
 CHUNK = 16
+PITCH = CHUNK + 1
 SPAN = PIX + 8
 WIDE = 2 * PIX
 MESH = pl.DeviceIdType.MESH
@@ -72,12 +73,12 @@
     def work(c, _):
         fetch(c).wait()
         for a in range(PIX):
-            spread[a * CHUNK : (a + 1) * CHUNK, :] = raw[c, :, a * PIX : (a + 1) * PIX].astype(
+            spread[a * PITCH : a * PITCH + CHUNK, :] = raw[c, :, a * PIX : (a + 1) * PIX].astype(
                 jnp.float32
             )
         for j in range(CHUNK):
             t = c * CHUNK + j
-            grid = spread[pl.ds(j, PIX, stride=CHUNK), :].astype(jnp.bfloat16)
+            grid = spread[pl.ds(j, PIX, stride=PITCH), :].astype(jnp.bfloat16)
             part = jnp.dot(grid, col_maps[visit[t]], preferred_element_type=jnp.float32)
             high, low = in_two(weight[t] * (part[:, :PIX] + part[:, PIX:]))
             mid[j, :PIX, :] = high
@@ -284,7 +285,7 @@
         out_specs=(VMEM, VMEM, VMEM),
         scratch_shapes=[
             pltpu.VMEM((count // CHUNK, CHUNK, PIX * PIX), bf16),
-            pltpu.VMEM((PIX * CHUNK, PIX), f32),
+            pltpu.VMEM((PIX * PITCH, PIX), f32),
             pltpu.VMEM((CHUNK, 3 * PIX, PIX), bf16),
             pltpu.VMEM((visits, SPAN + 8, 3 * PIX), bf16),
             pltpu.VMEM((visits, PIX, 2 * PIX), bf16),

time: 27.2 us -> 26.5 us (0.974)
  Pallas kernels: 26.3 us -> 25.6 us
    pallas_call x1, Pallas kernels: 8.15 us -> 7.48 us  [on_device(): pl.pallas_call(functools.partial(local_kernel, bands, visits), out_shape=...]
where the time goes in v3:
time: 26.5 us; the launch traced here: 26.3 us
  Pallas kernels  25.6 us (97%)
  between operations  0.65 us (2%)
    pallas_call x1, Pallas kernels, on_device(): pl.pallas_call(functools.partial(reduce_kernel, bands, decs, visits), out...  16.6 us
    pallas_call x1, Pallas kernels, on_device(): pl.pallas_call(functools.partial(local_kernel, bands, visits), out_shape=...  7.48 us
    pallas_call x1, Pallas kernels, on_device(): pl.pallas_call(divide_kernel, out_shape=(cell, cell), in_specs=[VMEM, VME...  1.53 us

profile of v3, /device:TPU:0, one launch (start us, length us, event | category | flops | bytes accessed | tf_op | source)
XLA Modules:
  0.0 26.3 jit_solution(18105826032657600359)
XLA Ops:
  0.6 7.5 %local_sums.1 = (f32[4,192,128]{2,1,0:T(8,128)}, f32[32,256]{1,0:T(8,128)}, f32[8,128]{1,0:T(8,128)}) custom-call(bf16[64,16384]{1,0:T(8,128)(2,1)} %tiles_hbm.1, s32[64]{0:T(128)} %bitcast.3, s32[64]{0:T(128)} %visit.1, s32[64]{0:T(128)} %offset.1, f32[64]{0:T(128)} %weight.1, f32[5,2,8]{2,1,0:T(2,128)} %bitcast.2, bf16[8,2,128,128]{3,2,1,0:T(8,128)(2,1)} %maps.1), custom_call_target="tpu_custom_call" | custom-call | tf_op jit(solution)/shard_map/local_sums/pallas_call | solution.py:277
  8.1 16.6 %reduce_cells.1 = (f32[128,128]{1,0:T(8,128)}, f32[128,128]{1,0:T(8,128)}) custom-call(f32[4,192,128]{2,1,0:T(8,128)} %get-tuple-element.7.num_in, f32[32,256]{1,0:T(8,128)} %get-tuple-element.8.den_in, f32[8,128]{1,0:T(8,128)} %get-tuple-element.9.cols), custom_call_target="tpu_custom_call" | custom-call | tf_op jit(solution)/shard_map/reduce_cells/pallas_call | solution.py:305
  24.8 1.5 %divide_cells.1 = (f32[128,128]{1,0:T(8,128)}, f32[128,128]{1,0:T(8,128)}) custom-call(f32[128,128]{1,0:T(8,128)} %get-tuple-element.10.num, f32[128,128]{1,0:T(8,128)} %get-tuple-element.11.den), custom_call_target="tpu_custom_call" | custom-call | tf_op jit(solution)/shard_map/divide_cells/pallas_call | solution.py:337
